TPU v7x, 32 devices: a whole 2x2x4 slice. The times are simulated.
32 devices in a mesh: region: 2 (over core), cells: 16 (over z, y, x).
Axes of the slice: x: 2, y: 2, z: 4, core: 2. Of those that a mesh axis runs over, the one named last changes fastest.
Arguments:
- moments: float32 [2, 6, 4, 128, 2048], P('region', None, None, None, 'cells'), may hold values from 0 to 40, as said below
- courant_azimuth: float32 [2, 4, 128, 2048], P('region', None, None, 'cells'), may hold values from 0.1 to 0.3
- courant_radial: float32 [2, 4, 128, 2048], P('region', None, None, 'cells'), may hold values from -0.25 to 0.25
- courant_axial: float32 [2, 4, 128, 2048], P('region', None, None, 'cells'), may hold values from -0.2 to 0.2
- shear: float32 [2, 4, 128, 2048], P('region', None, None, 'cells'), may hold values from 0.5 to 4
- owner: int32 [2, 2048, 1], P('region', 'cells'), may hold values from 0 to 15; in each aligned block of 128 rows (0 to 127, 128 to 255, ..., all dimensions but the last counted through in order) at most 16 rows name the same one
- target: int32 [2, 2048], P('region', 'cells'), may hold values from 0 to 127
- ami_weight: float32 [2, 2048, 128, 128], P('region', 'cells'), may hold values from 0 to 1, as said below
Outputs:
- updated: float32 [2, 6, 4, 128, 2048], P('region', None, None, None, 'cells')
Inputs may be any that keep to these rules, and one draw needn't show every extreme that they name: The rows of one device name each owner at most 16 times. Each cell's six entries are the moments of orders 0 to 5 of a positive measure on three or more sizes between 0.3 and 1.6. `ami_weight`: all entries are nonnegative.
All inputs are finite; a program needn't handle non-finite values.
Results may differ from a plain program's by a relative error of at most 0.0003.
Values sent between devices are 32-bit elements; how exact they have to be, the bound alone decides.
No kernel may reach another device: no remote copies, remote signals or barrier semaphores. Data moves between devices by JAX's collectives and lax.ppermute only.
A program may use at most 64 MiB of HBM per device.

v0:
```python
import math

import jax
import jax.numpy as jnp
from jax import lax
from jax.sharding import PartitionSpec as P

KAGG = 0.005
KBRK = 0.02


def from_partner(shard, axis, bit):
    return lax.ppermute(shard, axis, [(i, i ^ 1 << bit) for i in range(lax.axis_size(axis))])


def shifted(shard, axis, by):
    count = lax.axis_size(axis)
    return lax.ppermute(shard, axis, [(i, (i + by) % count) for i in range(count)])


def quadrature(moment):
    mass = moment[0]
    scaled = [moment[degree] / mass for degree in range(6)]
    mean_size = scaled[1]
    first_two = scaled[2] - mean_size * scaled[1]
    first_three = scaled[3] - mean_size * scaled[2]
    first_four = scaled[4] - mean_size * scaled[3]
    first_five = scaled[5] - mean_size * scaled[4]
    alpha_one = first_three / first_two - mean_size
    second_two = first_four - alpha_one * first_three - first_two * scaled[2]
    second_three = first_five - alpha_one * first_four - first_two * scaled[3]
    alpha_two = second_three / second_two - first_three / first_two
    beta_two = second_two / first_two
    centre = (mean_size + alpha_one + alpha_two) / 3.0
    dev_zero = mean_size - centre
    dev_one = alpha_one - centre
    dev_two = alpha_two - centre
    spread = jnp.sqrt(
        (dev_zero * dev_zero + dev_one * dev_one + dev_two * dev_two + 2.0 * (first_two + beta_two))
        / 6.0
    )
    determ = dev_zero * (dev_one * dev_two - beta_two) - first_two * dev_two
    cosine = jnp.clip(determ / (2.0 * spread * spread * spread), -1.0, 1.0)
    third = jnp.arccos(cosine) / 3.0
    node_high = centre + 2.0 * spread * jnp.cos(third)
    node_low = centre + 2.0 * spread * jnp.cos(third + 2.0 * math.pi / 3.0)
    node_mid = 3.0 * centre - node_high - node_low
    nodes = [node_low, node_mid, node_high]
    weights = []
    for node in nodes:
        lead = node - mean_size
        trail = (node - alpha_one) * lead - first_two
        norm_sq = 1.0 + lead * lead / first_two + trail * trail / (first_two * beta_two)
        weights.append(mass / norm_sq)
    return (nodes, weights)


def sources(moment, shear):
    nodes, weights = quadrature(moment)
    cubes = [node * node * node for node in nodes]
    pairs = []
    for first in range(3):
        for second in range(3):
            summed = nodes[first] + nodes[second]
            kernel = shear * summed * summed * summed
            pairs.append(
                (
                    first,
                    second,
                    weights[first] * weights[second] * kernel,
                    jnp.log(cubes[first] + cubes[second]),
                )
            )
    result = []
    for degree in range(6):
        birth = jnp.zeros_like(shear)
        death = jnp.zeros_like(shear)
        for first, second, pair, logsum in pairs:
            birth = birth + 0.5 * pair * jnp.exp(degree / 3.0 * logsum)
            death = death + pair * nodes[first] ** degree
        factor = 2.0 ** (1.0 - degree / 3.0) - 1.0
        breakage = jnp.zeros_like(shear)
        for index in range(3):
            breakage = (
                breakage
                + weights[index] * KBRK * shear * cubes[index] * factor * nodes[index] ** degree
            )
        result.append(moment[degree] + KAGG * (birth - death) + breakage)
    return jnp.stack(result)


def advance(moment, previous, ghost_layer, is_rotor, azim, radial, axial, shear):
    empty_layer = jnp.zeros_like(ghost_layer)
    beyond_edge = jnp.where(is_rotor, ghost_layer, empty_layer)
    below_edge = jnp.where(is_rotor, empty_layer, ghost_layer)
    prev_azim = jnp.concatenate([previous[..., None], moment[..., :-1]], axis=3)
    radial_below = jnp.concatenate([below_edge[:, None], moment[:, :-1]], axis=1)
    radial_beyond = jnp.concatenate([moment[:, 1:], beyond_edge[:, None]], axis=1)
    axial_pad = jnp.zeros_like(moment[:, :, :1])
    axial_below = jnp.concatenate([axial_pad, moment[:, :, :-1]], axis=2)
    axial_beyond = jnp.concatenate([moment[:, :, 1:], axial_pad], axis=2)
    advected = (
        moment
        - azim * (moment - prev_azim)
        - jnp.maximum(radial, 0.0) * (moment - radial_below)
        - jnp.minimum(radial, 0.0) * (radial_beyond - moment)
        - jnp.maximum(axial, 0.0) * (moment - axial_below)
        - jnp.minimum(axial, 0.0) * (axial_beyond - moment)
    )
    return sources([advected[degree] for degree in range(6)], shear)


def collect(received, received_rows, row_count):
    hits = (jnp.arange(row_count)[:, None] == received_rows[None, :]).astype(jnp.float32)
    summed = jnp.dot(
        hits, received, precision=lax.Precision.HIGHEST, preferred_element_type=jnp.float32
    )
    return summed.reshape(row_count, 6, -1).transpose(1, 0, 2)


def on_device(
    moments, courant_azimuth, courant_radial, courant_axial, shear, owner, target, ami_weight
):
    moment = moments[0]
    layer_count = moment.shape[1]
    row_count = moment.shape[2]
    face_count = moment.shape[3]
    peers = lax.axis_size("cells")
    capacity = max(2, 2 * row_count // peers)
    is_rotor = lax.axis_index("region") == 0
    layer = jnp.where(is_rotor, moment[:, layer_count - 1], moment[:, 0])
    contrib = jnp.einsum("zfg,kzg->zkf", ami_weight[0], layer, precision=lax.Precision.HIGHEST)
    owners = owner[0, :, 0]
    rows_to = target[0]
    order_idx = jnp.arange(row_count)
    same_owner = owners[:, None] == owners[None, :]
    earlier = order_idx[None, :] < order_idx[:, None]
    rank = jnp.sum(jnp.logical_and(same_owner, earlier).astype(jnp.int32), axis=1)
    destination = owners * capacity + rank
    slot_ids = jnp.arange(peers * capacity)
    picked = slot_ids[:, None] == destination[None, :]
    outgoing = jnp.dot(
        picked.astype(jnp.float32),
        contrib.reshape(row_count, 6 * face_count),
        precision=lax.Precision.HIGHEST,
        preferred_element_type=jnp.float32,
    )
    outgoing_rows = jnp.sum(jnp.where(picked, rows_to[None, :], 0), axis=1)
    received, received_rows = (
        lax.all_to_all(outgoing, "cells", split_axis=0, concat_axis=0, tiled=True),
        lax.all_to_all(outgoing_rows, "cells", split_axis=0, concat_axis=0, tiled=True),
    )
    other_ghost = collect(received, received_rows, row_count)
    ghost_layer = from_partner(other_ghost, "region", 0)
    rim = moment[:, :, :, face_count - 1]
    previous = shifted(rim, "cells", 1)
    updated = advance(
        moment,
        previous,
        ghost_layer,
        is_rotor,
        courant_azimuth[0],
        courant_radial[0],
        courant_axial[0],
        shear[0],
    )
    return updated[None]


def solution(mesh):
    placed = (
        P("region", None, None, None, "cells"),
        P("region", None, None, "cells"),
        P("region", None, None, "cells"),
        P("region", None, None, "cells"),
        P("region", None, None, "cells"),
        P("region", "cells", None),
        P("region", "cells"),
        P("region", "cells", None, None),
    )
    return jax.shard_map(
        on_device,
        mesh=mesh,
        in_specs=placed,
        out_specs=P("region", None, None, None, "cells"),
        check_vma=False,
    )
```

profile of v0, /device:TPU:1, one launch (start us, length us, event | category | flops | bytes accessed | tf_op | source)
XLA Modules:
  0.0 76.1 jit_solution(894927941815311553)
XLA Ops:
  0.0 0.9 %convert_reduce_fusion = s32[128]{0:T(128)S(1)} fusion(s32[128]{0:T(128)} %bitcast.57), kind=kLoop, calls=%fused_computation.176 | loop fusion | flops 81792 | bytes 1024 | tf_op jit(solution)/shard_map/reduce_sum | solution.py:138
  0.9 0.7 multiply_add_fusion.4
  1.6 0.8 %select_reduce_fusion = s32[256]{0:T(256)S(1)} fusion(s32[128]{0:T(128)} %bitcast.56, s32[128]{0:T(128)S(1)} %multiply_add_fusion.4), kind=kLoop, calls=%fused_computation.167 | loop fusion | flops 98048 | bytes 2048 | tf_op jit(solution)/shard_map/reduce_sum | solution.py:148
  2.3 0.7 all_to_all.12
  3.0 7.4 %all-to-all-start = ((s32[16,16,1]{1,2,0:T(1,128)}), s32[16,16,1]{1,2,0:T(1,128)S(1)}, u32[]{:S(2)}, u32[]{:S(2)}) async-start(s32[16,16,1]{1,2,0:T(1,128)} %bitcast.6), calls=%async_computation | async-start | bytes 16384 | tf_op jit(solution)/shard_map/all_to_all | solution.py:151
  10.5 1.2 %fusion.11 = f32[6,128,128]{2,1,0:T(8,128)S(1)} fusion(f32[6,4,128,128]{3,2,1,0:T(8,128)} %bitcast.46, pred[]{:T(512)S(6)} %eq.61), kind=kLoop, calls=%fused_computation.17 | loop fusion | flops 98304 | bytes 1179649 | tf_op jit(solution)/shard_map/jit(_where)/select_n | solution.py:131
  11.6 15.4 %fusion = f32[128,6,128]{2,1,0:T(8,128)S(1)} fusion(f32[1,128,128,128]{3,2,1,0:T(8,128)} %param.15, f32[6,128,128]{2,1,0:T(8,128)S(1)} %fusion.11), kind=kOutput, calls=%fused_computation | convolution fusion | flops 150994944 | bytes 9175040 | tf_op jit(solution)/shard_map/zfg,kzg->zkf/dot_general | solution.py:132
  27.3 1.4 %fusion.105 = f32[16,16,768]{2,1,0:T(8,128)} fusion(f32[128,768,1]{0,1,2:T(8,128)S(1)} %bitcast.53, s32[128]{0:T(128)S(1)} %multiply_add_fusion.4, s32[16,16]{1,0:T(8,128)S(1)} %multiply_add_fusion.3), kind=kOutput, calls=%fused_computation.171 | convolution fusion | flops 302022656 | bytes 1181184 | tf_op jit(solution)/shard_map/dot_general | solution.py:142
  28.7 6.3 %all-to-all-start.1 = ((f32[16,16,768]{2,1,0:T(8,128)}), f32[16,16,768]{2,1,0:T(8,128)S(1)}, u32[]{:S(2)}, u32[]{:S(2)}) async-start(f32[16,16,768]{2,1,0:T(8,128)} %fusion.105), calls=%async_computation.1 | async-start | bytes 1572864 | tf_op jit(solution)/shard_map/all_to_all | solution.py:150
  35.0 0.9 %slice_reduce_fusion = f32[6,4,128]{2,1,0:T(4,128)S(1)} fusion(f32[6,4,128,128]{3,2,1,0:T(8,128)S(1)} %bitcast.47), kind=kLoop, calls=%fused_computation.2 | loop fusion | bytes 24576 | tf_op jit(solution)/shard_map/slice | solution.py:155
  36.0 1.6 %collective-permute-start = (f32[6,4,128]{2,1,0:T(4,128)S(1)}, f32[6,4,128]{2,1,0:T(4,128)S(1)}, u32[]{:S(2)}, u32[]{:S(2)}) collective-permute-start(f32[6,4,128]{2,1,0:T(4,128)S(1)} %slice_reduce_fusion), channel_id=1, source_target_pairs={{0,1},{1,2},{2,3},{3,4},{4,5},{5,6},{6,7},{7,8},{8,9},{9,10},{10,1... | collective-permute-start | bytes 36872 | tf_op jit(solution)/shard_map/ppermute | solution.py:18
  37.6 2.0 %fusion.120 = (f32[6,4,127,128]{3,2,1,0:T(8,128)}, f32[6,4,127,128]{3,2,1,0:T(8,128)}) fusion(f32[6,4,128,128]{3,2,1,0:T(8,128)S(1)} %bitcast.48), kind=kLoop, calls=%fused_computation.181 | loop fusion | bytes 6242304 | tf_op jit(solution)/shard_map/slice | solution.py:100
  39.5 0.6 broadcast.324
  40.1 0.7 reduce.5
  40.9 12.0 %all-to-all-done.1 = f32[16,16,768]{2,1,0:T(8,128)S(1)} async-done(((f32[16,16,768]{2,1,0:T(8,128)}), f32[16,16,768]{2,1,0:T(8,128)S(1)}, u32[]{:S(2)}, u32[]{:S(2)}) %all-to-all-start.1) | async-done | bytes 786464 | tf_op jit(solution)/shard_map/all_to_all | solution.py:150
  53.2 1.3 %convolution_bitcast_fusion = f32[6,128,128]{2,1,0:T(8,128)} fusion(f32[6,128,256]{2,1,0:T(8,128)S(1)} %bitcast.52, s32[256]{0:T(256)S(1)} %eq.69), kind=kOutput, calls=%fused_computation.14 | convolution fusion | flops 302022656 | bytes 1180672 | tf_op jit(solution)/shard_map/dot_general | solution.py:115
  54.5 3.1 %collective-permute-start.1 = (f32[6,128,128]{2,1,0:T(8,128)}, f32[6,128,128]{2,1,0:T(8,128)}, u32[]{:S(2)}, u32[]{:S(2)}) collective-permute-start(f32[6,128,128]{2,1,0:T(8,128)} %convolution_bitcast_fusion), channel_id=1, source_target_pairs={{0,16},{16,0},{1,17},{17,1},{2,18},{18,2},{3,19},{19,3},{4,20},{20... | collective-permute-start | bytes 1179656 | tf_op jit(solution)/shard_map/ppermute | solution.py:13
  57.5 1.7 %fusion.121 = (f32[6,3,128,128]{3,2,1,0:T(8,128)}, f32[6,3,128,128]{3,2,1,0:T(8,128)}) fusion(f32[6,4,128,128]{3,2,1,0:T(8,128)S(1)} %bitcast.49), kind=kLoop, calls=%fused_computation.182 | loop fusion | bytes 4718592 | tf_op jit(solution)/shard_map/slice | solution.py:98
  59.2 1.0 %maximum_bitcast_fusion = (f32[4,128,128]{2,1,0:T(8,128)S(1)}, f32[4,128,128]{2,1,0:T(8,128)}, f32[4,128,128]{2,1,0:T(8,128)}, f32[4,128,128]{2,1,0:T(8,128)}) fusion(f32[1,4,128,128]{3,2,1,0:T(8,128)S(1)} %copy-done.3, f32[1,4,128,128]{3,2,1,0:T(8,128)S(1)} %copy-done.4), kind=kLoop, calls=%fused_computation.158 | loop fusion | flops 262144 | bytes 1572864 | tf_op jit(solution)/shard_map/mul | solution.py:107
  60.2 0.5 copy.36
  60.7 1.2 %select_bitcast_fusion = (f32[6,1,128,128]{3,2,1,0:T(8,128)S(1)}, f32[6,1,128,128]{3,2,1,0:T(8,128)S(1)}) fusion(f32[6,128,128]{2,1,0:T(8,128)} %collective-permute-done.1, pred[]{:T(512)S(6)} %eq.61), kind=kLoop, calls=%fused_computation.25 | loop fusion | flops 196608 | bytes 1179649 | tf_op jit(solution)/shard_map/broadcast_in_dim | solution.py:98
  62.1 3.8 %fusion.7 = f32[6,4,128,128]{3,2,1,0:T(8,128)S(1)} fusion(f32[6,4,128,127]{3,2,1,0:T(8,128)S(1)} %bitcast.50, f32[6,4,128,1]{3,2,1,0:T(8,128)S(1)} %copy.36, f32[6,3,128,128]{3,2,1,0:T(8,128)} %get-tuple-element.29, f32[6,1,128,128]{3,2,1,0:T(8,128)S(1)} %get-tuple-element.31, f32[6,1,128,128]{3,2,1,0:T(8,128)S(1)} %get-tuple-element.30, ...), kind=kLoop, calls=%fused_computation.9 | loop fusion | flops 7077888 | bytes 12296192 | tf_op jit(solution)/shard_map/sub | solution.py:103
  66.1 3.0 %add_divide_fusion.1 = (f32[1,4,128,128]{3,2,1,0:T(8,128)S(1)}, f32[1,4,128,128]{3,2,1,0:T(8,128)S(1)}, f32[1,4,128,128]{3,2,1,0:T(8,128)S(1)}, f32[1,4,128,128]{3,2,1,0:T(8,128)S(1)}, f32[1,4,128,128]{3,2,1,0:T(8,128)S(1)}) fusion(f32[1,4,128,128]{3,2,1,0:T(8,128)S(1)} %get-tuple-element.22, f32[1,4,128,128]{3,2,1,0:T(8,128)S(1)} %get-tuple-element.21, ...), kind=kLoop, calls=%fused_computation.145 | loop fusion | flops 3997696 | bytes 3145728 | tf_op jit(solution)/shard_map/div | solution.py:54
  69.1 0.3 add_divide_fusion
  69.4 0.6 copy-done.2
  70.0 1.0 %add_dynamic-update-slice_fusion = (f32[6,4,128,128]{3,2,1,0:T(8,128)S(1)}, f32[1,4,128,128]{3,2,1,0:T(8,128)S(1)}, f32[1,4,128,128]{3,2,1,0:T(8,128)S(1)}, f32[...) fusion(f32[1,4,128,128]{3,2,1,0:T(8,128)S(1)} %get-tuple-elemen, ...), kind=kLoop, calls=%fused_computation.127 | loop fusion | flops 6356991 | bytes 4718592
  71.1 0.8 %fusion.90 = f32[6,4,128,128]{3,2,1,0:T(8,128)S(1)} fusion(f32[6,4,128,128]{3,2,1,0:T(8,128)S(1)} %get-tuple-element.5, f32[1,4,128,128]{3,2,1,0:T(8,128)S(1)} %get-tuple-element.17, f32[1,4,128,128]{3,2,1,0:T(8,128)S(1)} %get-tuple-element.18, f32[1,4,128,128]{3,2,1,0:T(8,128)S(1)} %get-tuple-element.14, f32[1,4,128,128]{3,2,1,0:T(8,128)S(1)} %get-tuple-element.16, ...), kind=kLoop, calls=%fused_computation.126 | loop fusion | flops 4259840 | bytes 3670016
  71.9 0.8 %fusion.48 = f32[6,4,128,128]{3,2,1,0:T(8,128)S(1)} fusion(f32[6,4,128,128]{3,2,1,0:T(8,128)S(1)} %fusion.90, f32[1,4,128,128]{3,2,1,0:T(8,128)S(1)} %get-tuple-element.7, f32[1,4,128,128]{3,2,1,0:T(8,128)S(1)} %get-tuple-element.16, f32[1,4,128,128]{3,2,1,0:T(8,128)S(1)} %get-tuple-element.8, f32[1,4,128,128]{3,2,1,0:T(8,128)S(1)} %get-tuple-element.10, ...), kind=kLoop, calls=%fused_computation.81 | loop fusion | flops 4259840 | bytes 3670016
  72.6 0.7 fusion.80
  73.4 0.8 %fusion.32 = f32[6,4,128,128]{3,2,1,0:T(8,128)S(1)} fusion(f32[6,4,128,128]{3,2,1,0:T(8,128)S(1)} %fusion.80, f32[1,4,128,128]{3,2,1,0:T(8,128)S(1)} %get-tuple-element.9, f32[1,4,128,128]{3,2,1,0:T(8,128)S(1)} %get-tuple-element.18, f32[1,4,128,128]{3,2,1,0:T(8,128)S(1)} %get-tuple-element.10, f32[1,4,128,128]{3,2,1,0:T(8,128)S(1)} %get-tuple-element.11, ...), kind=kLoop, calls=%fused_computation.65 | loop fusion | flops 4456448 | bytes 3670016
  74.2 0.8 %fusion.70 = f32[6,4,128,128]{3,2,1,0:T(8,128)S(1)} fusion(f32[6,4,128,128]{3,2,1,0:T(8,128)S(1)} %fusion.32, f32[1,4,128,128]{3,2,1,0:T(8,128)S(1)} %get-tuple-element.14, f32[1,4,128,128]{3,2,1,0:T(8,128)S(1)} %get-tuple-element.12, f32[1,4,128,128]{3,2,1,0:T(8,128)S(1)} %get-tuple-element.17, f32[1,4,128,128]{3,2,1,0:T(8,128)S(1)} %get-tuple-element.13, ...), kind=kLoop, calls=%fused_computation.104 | loop fusion | flops 4653056 | bytes 3670016 | tf_op jit(solution)/shard_map/stack | solution.py:89
  75.0 1.1 %copy-done.5 = f32[6,4,128,128]{3,2,1,0:T(8,128)} copy-done((f32[6,4,128,128]{3,2,1,0:T(8,128)}, f32[6,4,128,128]{3,2,1,0:T(8,128)S(1)}, u32[]{:S(2)}) %copy-start.5) | copy-done | bytes 1572888
  (18 shorter events, 1.1 us)
Async XLA Ops:
  3.0 25.7 %all-to-all-start = ((s32[16,16,1]{1,2,0:T(1,128)}), s32[16,16,1]{1,2,0:T(1,128)S(1)}, u32[]{:S(2)}, u32[]{:S(2)}) async-start(s32[16,16,1]{1,2,0:T(1,128)} %bitcast.6), calls=%async_computation | async-start | bytes 16384 | tf_op jit(solution)/shard_map/all_to_all | solution.py:151
  27.3 7.8 %copy-start = (f32[1,6,4,128,128]{4,3,2,1,0:T(8,128)S(1)}, f32[1,6,4,128,128]{4,3,2,1,0:T(8,128)}, u32[]{:S(2)}) copy-start(f32[1,6,4,128,128]{4,3,2,1,0:T(8,128)} %param.8) | copy-start | bytes 4718596
  28.7 24.2 %all-to-all-start.1 = ((f32[16,16,768]{2,1,0:T(8,128)}), f32[16,16,768]{2,1,0:T(8,128)S(1)}, u32[]{:S(2)}, u32[]{:S(2)}) async-start(f32[16,16,768]{2,1,0:T(8,128)} %fusion.105), calls=%async_computation.1 | async-start | bytes 1572864 | tf_op jit(solution)/shard_map/all_to_all | solution.py:150
  36.0 24.2 %collective-permute-start = (f32[6,4,128]{2,1,0:T(4,128)S(1)}, f32[6,4,128]{2,1,0:T(4,128)S(1)}, u32[]{:S(2)}, u32[]{:S(2)}) collective-permute-start(f32[6,4,128]{2,1,0:T(4,128)S(1)} %slice_reduce_fusion), channel_id=1, source_target_pairs={{0,1},{1,2},{2,3},{3,4},{4,5},{5,6},{6,7},{7,8},{8,9},{9,10},{10,1... | collective-permute-start | bytes 36872 | tf_op jit(solution)/shard_map/ppermute | solution.py:18
  54.5 4.7 %copy-start.3 = (f32[1,4,128,128]{3,2,1,0:T(8,128)S(1)}, f32[1,4,128,128]{3,2,1,0:T(8,128)}, u32[]{:S(2)}) copy-start(f32[1,4,128,128]{3,2,1,0:T(8,128)} %param.11) | copy-start | bytes 786436
  54.5 4.7 %copy-start.4 = (f32[1,4,128,128]{3,2,1,0:T(8,128)S(1)}, f32[1,4,128,128]{3,2,1,0:T(8,128)}, u32[]{:S(2)}) copy-start(f32[1,4,128,128]{3,2,1,0:T(8,128)} %param.10) | copy-start | bytes 786436
  54.5 6.2 %collective-permute-start.1 = (f32[6,128,128]{2,1,0:T(8,128)}, f32[6,128,128]{2,1,0:T(8,128)}, u32[]{:S(2)}, u32[]{:S(2)}) collective-permute-start(f32[6,128,128]{2,1,0:T(8,128)} %convolution_bitcast_fusion), channel_id=1, source_target_pairs={{0,16},{16,0},{1,17},{17,1},{2,18},{18,2},{3,19},{19,3},{4,20},{20... | collective-permute-start | bytes 1179656 | tf_op jit(solution)/shard_map/ppermute | solution.py:13
  60.7 1.4 %copy-start.1 = (f32[6,3,128,128]{3,2,1,0:T(8,128)S(1)}, f32[6,3,128,128]{3,2,1,0:T(8,128)}, u32[]{:S(2)}) copy-start(f32[6,3,128,128]{3,2,1,0:T(8,128)} %get-tuple-element.28) | copy-start | bytes 3538948
  69.1 1.0 %copy-start.2 = (f32[1,4,128,128]{3,2,1,0:T(8,128)S(1)}, f32[1,4,128,128]{3,2,1,0:T(8,128)}, u32[]{:S(2)}) copy-start(f32[1,4,128,128]{3,2,1,0:T(8,128)} %param.12) | copy-start | bytes 786436
  75.0 1.1 %copy-start.5 = (f32[6,4,128,128]{3,2,1,0:T(8,128)}, f32[6,4,128,128]{3,2,1,0:T(8,128)S(1)}, u32[]{:S(2)}) copy-start(f32[6,4,128,128]{3,2,1,0:T(8,128)S(1)} %fusion.70) | copy-start | bytes 4718596
where the time goes:
time: 76.5 us; the launch traced here: 76.1 us
  other arithmetic  18.6 us (24%)
  starting transfers between devices  18.4 us (24%)
  matrix products  18.1 us (24%)
  waiting for transfers between devices  12 us (16%)
  local copies, waits for them, and re-layouts  8.86 us (12%)
    dot_general x1, matrix products, on_device(): jnp.einsum('zfg,kzg->zkf', ami_weight[0], layer, precision=lax.Precision....  15.4 us
    all_to_all x1, waiting for transfers between devices, on_device(): lax.all_to_all(outgoing, 'cells', split_axis=0, concat_axis=0, tiled=True)  12 us
    all_to_all x1, starting transfers between devices, on_device(): lax.all_to_all(outgoing_rows, 'cells', split_axis=0, concat_axis=0, tiled...  7.4 us
    all_to_all x1, starting transfers between devices, on_device(): lax.all_to_all(outgoing, 'cells', split_axis=0, concat_axis=0, tiled=True)  6.34 us
    unnamed x5, other arithmetic  4.14 us
    sub x1, other arithmetic, advance(): moment - azim * (moment - prev_azim)  3.78 us
    div x2, other arithmetic, quadrature(): weights.append(mass / norm_sq)  3.25 us
    ppermute x1, starting transfers between devices, from_partner(): lax.ppermute(shard, axis, [(i, i ^ 1 << bit) for i in range(lax.axis_size...  3.06 us
  transfers between devices with their start and end apart: 4, of which 1 were waited for; matrix products, arithmetic and copies ran while one was open for 36% of the time, Pallas kernels for 0%

commit v1 on v0

v1 whole, which is shorter than its diff:
```python
import functools
import math

import jax
import jax.numpy as jnp
from jax import lax
from jax.experimental import pallas as pl
from jax.experimental.pallas import tpu as pltpu
from jax.sharding import PartitionSpec as P


KAGG = 0.005
KBRK = 0.02
ORDERS = 6
F32 = jnp.float32
BF16 = jnp.bfloat16
KERNEL_VMEM = 8 * 1024 * 1024
PAD = 8
GROUP = 8
TILE = 32
FULL_VMEM = 58 * 1024 * 1024
BOUNDS = (0, 4, 8, 12, 14, 16)
IN_VMEM = pl.BlockSpec(memory_space=pltpu.VMEM)
IN_HBM = pl.BlockSpec(memory_space=pltpu.HBM)

COS_THIRD = (
    0.44444444535893496,
    0.04115211563399856,
    0.009758495429256357,
    0.0029417445898478234,
    0.0012216398155368902,
    -0.00013418618671007774,
    0.0009423656998505278,
    -0.000598812660480466,
    0.00027219066323123,
)


def two_parts(value):
    high = value.astype(BF16)
    return high, (value - high.astype(F32)).astype(BF16)


def quadrature(moment):
    inv_mass = 1.0 / moment[0]
    n1, n2, n3, n4, n5 = [moment[degree] * inv_mass for degree in range(1, 6)]
    p1 = n2 - n1 * n1
    p2 = n3 - n1 * n2
    p3 = n4 - n1 * n3
    p4 = n5 - n1 * n4
    inv_p1 = 1.0 / p1
    slope = p2 * inv_p1
    a1 = slope - n1
    q2 = p3 - a1 * p2 - p1 * n2
    q3 = p4 - a1 * p3 - p1 * n3
    inv_q2 = 1.0 / q2
    a2 = q3 * inv_q2 - slope
    b2 = q2 * inv_p1
    centre = (n1 + a1 + a2) * (1.0 / 3.0)
    d0 = n1 - centre
    d1 = a1 - centre
    d2 = a2 - centre
    square = (d0 * d0 + d1 * d1 + d2 * d2 + 2.0 * (p1 + b2)) * (1.0 / 6.0)
    inv_h = lax.rsqrt(square)
    h = square * inv_h
    determ = d0 * (d1 * d2 - b2) - p1 * d2
    cosine = jnp.clip(determ * 0.5 * (inv_h * inv_h * inv_h), -1.0, 1.0)
    half = jnp.sqrt(0.5 + 0.5 * cosine)
    w = (0.5 - 0.5 * cosine) / (1.0 + half)
    q = jnp.full_like(w, COS_THIRD[-1])
    for term in COS_THIRD[-2::-1]:
        q = q * w + term
    drop = w * q
    h_cos = h * (1.0 - drop)
    h_sin = h * jnp.sqrt(drop * (2.0 - drop)) * math.sqrt(3.0)
    high = centre + 2.0 * h_cos
    low = centre - h_cos - h_sin
    mid = 3.0 * centre - high - low
    nodes = (low, mid, high)
    weights = []
    for node in nodes:
        u = node - n1
        v = (node - a1) * u - p1
        weights.append(moment[0] / (1.0 + u * u * inv_p1 + v * v * inv_q2))
    return nodes, weights


def sources(moment, shear):
    nodes, weights = quadrature(moment)
    cubes = [node * node * node for node in nodes]
    rate = KBRK * shear
    agg = KAGG * shear
    breaks = [weights[i] * rate * cubes[i] for i in range(3)]
    equal = [weights[i] * agg * (4.0 * cubes[i]) * weights[i] for i in range(3)]
    lost = [2.0 * equal[i] for i in range(3)]
    pairs = []
    for i, j in ((0, 1), (0, 2), (1, 2)):
        summed = nodes[i] + nodes[j]
        pair = weights[i] * weights[j] * (agg * summed * summed * summed)
        lost[i] = lost[i] + pair
        lost[j] = lost[j] + pair
        volume = cubes[i] + cubes[j]
        root = jnp.exp(jnp.log(volume) * (1.0 / 3.0))
        pairs.append((pair, root, volume))
    updated = []
    node_powers = [jnp.ones_like(shear)] * 3
    for degree in range(ORDERS):
        grow = 2.0 ** (degree / 3.0)
        split = 2.0 ** (1.0 - degree / 3.0) - 1.0
        total = moment[degree]
        for i in range(3):
            net = grow * equal[i] - lost[i]
            if degree != 3:
                net = net + split * breaks[i]
            if degree > 0:
                net = net * node_powers[i]
            total = total + net
        for pair, root, volume in pairs:
            factor = (None, root, root * root, volume, volume * root, volume * root * root)[degree]
            total = total + (pair if factor is None else pair * factor)
        updated.append(total)
        node_powers = [power * node for power, node in zip(node_powers, nodes)] if degree else list(nodes)
    return updated


def dispatch_body(
    cap, owner_hbm, target_hbm, moments_hbm, weight_hbm, out, rim,
    moments, weight, source, ids, owner, target, count, index_sem, moment_sem, weight_sem,
):
    layers, rows, faces = moments.shape[1:]
    peers = count.shape[0]
    block = ORDERS * cap + 1
    rotor = lax.axis_index("region") == 0
    layer = jnp.where(rotor, layers - 1, 0)

    def layer_copy(index):
        which = jnp.where(rotor, layers - 1 - index, index)
        return pltpu.make_async_copy(moments_hbm.at[:, which], moments.at[:, which], moment_sem.at[index])

    def weight_copy(step):
        part = pl.ds(BOUNDS[step] * rows // BOUNDS[-1], (BOUNDS[step + 1] - BOUNDS[step]) * rows // BOUNDS[-1])
        return pltpu.make_async_copy(weight_hbm.at[part], weight.at[part], weight_sem.at[step])

    index_copies = (
        pltpu.make_async_copy(owner_hbm, owner, index_sem.at[0]),
        pltpu.make_async_copy(target_hbm, target, index_sem.at[1]),
    )
    layer_copy(0).start()
    for copy in index_copies:
        copy.start()
    for step in range(len(BOUNDS) - 1):
        weight_copy(step).start()
        if step == 0:
            for index in range(1, layers):
                layer_copy(index).start()

    out[...] = jnp.zeros_like(out)
    lane = lax.broadcasted_iota(jnp.int32, (1, faces), 1)
    offset = (lax.axis_index("cells") * cap) % faces
    mine = jnp.logical_and(lane >= offset, lane < offset + cap)
    ids[...] = jnp.broadcast_to(jnp.where(mine, -1.0, 0.0), ids.shape)

    @pl.loop(0, peers)
    def _(peer):
        count[peer] = 0

    source[pl.ds(ORDERS * rows, (PAD - ORDERS) * rows)] = jnp.zeros(((PAD - ORDERS) * rows, faces), F32)
    layer_copy(0).wait()
    for degree in range(ORDERS):
        source[pl.ds(degree * rows, rows)] = moments[degree, layer]
    for copy in index_copies:
        copy.wait()
    width = PAD * GROUP
    column = (lax.broadcasted_iota(jnp.int32, (faces, 2 * width), 1) % width) // PAD
    turned = []
    for first in range(0, rows, GROUP):
        value = jnp.concatenate([source[pl.ds(first + i, PAD, stride=rows)] for i in range(GROUP)], axis=0)
        high = value.astype(BF16).astype(F32)
        turned.append(jnp.concatenate([high, value - high], axis=0).T)

    def place(first, product):
        product = product.T
        product = product[:width] + product[width:]
        for i in range(GROUP):
            peer = owner[first + i]
            rank = count[peer]
            count[peer] = rank + 1
            out[pl.ds(peer * block + rank * ORDERS, ORDERS), :] = product[PAD * i : PAD * i + ORDERS]
            ids[pl.ds(peer, 1), :] = jnp.where(
                lane == offset + rank, target[first + i].astype(F32), ids[pl.ds(peer, 1), :]
            )

    pending = []
    for step in range(len(BOUNDS) - 1):
        weight_copy(step).wait()
        products = []
        for group in range(BOUNDS[step], BOUNDS[step + 1]):
            first = group * GROUP
            rhs = jnp.concatenate([jnp.where(column == i, turned[group], 0.0).astype(BF16) for i in range(GROUP)], axis=0)
            parts = [two_parts(weight[first + i]) for i in range(GROUP)]
            product = sum(
                jnp.dot(jnp.concatenate([part[which] for part in parts], axis=1), rhs, preferred_element_type=F32)
                for which in range(2)
            )
            products.append((first, product))
            if pending:
                place(*pending.pop(0))
        if step == 0:
            for index in range(1, layers):
                layer_copy(index).wait()
            tail = jnp.zeros((rows, faces), F32)
            wide = lax.broadcasted_iota(jnp.int32, (rows, faces), 1)
            for degree in range(ORDERS):
                for which in range(layers):
                    spot = degree * layers + which
                    tail = jnp.where(wide == spot, pltpu.roll(moments[degree, which], spot + 1, 1), tail)
            rim[...] = tail.T[: ORDERS * layers]
        for item in pending:
            place(*item)
        pending = products
    for item in pending:
        place(*item)

    for peer in range(peers):
        out[pl.ds(peer * block + ORDERS * cap, 1), :] = ids[pl.ds(peer, 1), :]


def dispatch(owner, target, moments, weight, peers, cap):
    layers, rows, faces = moments.shape[1:]
    return pl.pallas_call(
        functools.partial(dispatch_body, cap),
        out_shape=(
            jax.ShapeDtypeStruct((peers * (ORDERS * cap + 1), faces), F32),
            jax.ShapeDtypeStruct((ORDERS * layers, rows), F32),
        ),
        in_specs=[IN_HBM] * 4,
        out_specs=(IN_VMEM, IN_VMEM),
        scratch_shapes=[
            pltpu.VMEM(moments.shape, F32),
            pltpu.VMEM((rows, faces, faces), F32),
            pltpu.VMEM((PAD * rows, faces), F32),
            pltpu.VMEM((peers, faces), F32),
            pltpu.SMEM((rows,), jnp.int32),
            pltpu.SMEM((rows,), jnp.int32),
            pltpu.SMEM((peers,), jnp.int32),
            pltpu.SemaphoreType.DMA((2,)),
            pltpu.SemaphoreType.DMA((layers,)),
            pltpu.SemaphoreType.DMA((len(BOUNDS) - 1,)),
        ],
        compiler_params=pltpu.CompilerParams(vmem_limit_bytes=FULL_VMEM),
        name="dispatch",
    )(owner, target, moments, weight)


def local_body(
    moments_hbm, rim, azim_hbm, radial_hbm, axial_hbm, shear_hbm, out, edge,
    moments, azim, radial, axial, shear, adv, result, sems, load_sems,
):
    layers, rows, faces = moments.shape[1:]
    loads = [
        pltpu.make_async_copy(source, target, load_sems.at[index])
        for index, (source, target) in enumerate(
            ((moments_hbm, moments), (azim_hbm, azim), (radial_hbm, radial), (axial_hbm, axial), (shear_hbm, shear))
        )
    ]
    for load in loads:
        load.start()
    for load in loads:
        load.wait()
    rotor = lax.axis_index("region") == 0
    interface = jnp.where(rotor, layers - 1, 0)
    row = lax.broadcasted_iota(jnp.int32, (rows, faces), 0)
    lane = lax.broadcasted_iota(jnp.int32, (rows, faces), 1)

    def advect(layer, target):
        ca = azim[layer]
        cr = radial[layer]
        cz = axial[layer]
        outward = jnp.maximum(cr, 0.0)
        inward = outward - cr
        upward = jnp.maximum(cz, 0.0)
        downward = upward - cz
        keep = 1.0 - ca - (outward + inward) - (upward + downward)
        outward = jnp.where(layer > 0, outward, 0.0)
        inward = jnp.where(layer < layers - 1, inward, 0.0)
        upward = jnp.where(row > 0, upward, 0.0)
        downward = jnp.where(row < rows - 1, downward, 0.0)
        below = jnp.maximum(layer - 1, 0)
        beyond = jnp.minimum(layer + 1, layers - 1)
        for degree in range(ORDERS):
            m = moments[degree, layer]
            prev = jnp.where(lane == 0, rim[degree, layer], pltpu.roll(m, 1, 1))
            target[degree] = (
                keep * m
                + ca * prev
                + outward * moments[degree, below]
                + inward * moments[degree, beyond]
                + upward * pltpu.roll(m, 1, 0)
                + downward * pltpu.roll(m, rows - 1, 0)
            )

    def store(index, layer):
        return pltpu.make_async_copy(result.at[index], out.at[:, layer], sems.at[index])

    @pl.loop(0, layers - 1)
    def _(index):
        layer = jnp.where(rotor, index, index + 1)
        advect(layer, adv)

        @pl.loop(0, rows // TILE)
        def _(step):
            part = pl.ds(pl.multiple_of(step * TILE, TILE), TILE)
            updated = sources([adv[degree, part] for degree in range(ORDERS)], shear[layer, part])
            for degree in range(ORDERS):
                result[index, degree, part] = updated[degree]

        store(index, layer).start()

    advect(interface, edge)
    outward = jnp.maximum(radial[interface], 0.0)
    edge[ORDERS] = jnp.where(rotor, outward - radial[interface], outward)
    edge[ORDERS + 1] = shear[interface]

    @pl.loop(0, layers - 1)
    def _(index):
        store(index, jnp.where(rotor, index, index + 1)).wait()


def local_update(moments, rim, azim, radial, axial, shear):
    layers, rows, faces = moments.shape[1:]
    return pl.pallas_call(
        local_body,
        out_shape=(
            jax.ShapeDtypeStruct(moments.shape, F32),
            jax.ShapeDtypeStruct((ORDERS + 2, rows, faces), F32),
        ),
        in_specs=[IN_HBM, IN_VMEM] + [IN_HBM] * 4,
        out_specs=(IN_HBM, IN_VMEM),
        scratch_shapes=[pltpu.VMEM(moments.shape, F32)]
        + [pltpu.VMEM(azim.shape, F32)] * 4
        + [
            pltpu.VMEM((ORDERS, rows, faces), F32),
            pltpu.VMEM((layers - 1, ORDERS, rows, faces), F32),
            pltpu.SemaphoreType.DMA((layers - 1,)),
            pltpu.SemaphoreType.DMA((5,)),
        ],
        compiler_params=pltpu.CompilerParams(vmem_limit_bytes=FULL_VMEM),
        name="local_update",
    )(moments, rim, azim, radial, axial, shear)


def collect_body(peers, cap, received, out, gathered):
    rows, faces = out.shape[1], out.shape[2]
    block = ORDERS * cap + 1
    per_row = faces // cap
    row_id = lax.broadcasted_iota(jnp.int32, (rows, faces), 0).astype(F32)
    hits = []
    for first in range(0, peers, per_row):
        ids = jnp.zeros((1, faces), F32)
        for peer in range(first, min(peers, first + per_row)):
            ids = ids + received[pl.ds(peer * block + ORDERS * cap, 1), :]
        hits.append((row_id == ids).astype(BF16))
    hits = jnp.concatenate(hits, axis=1)
    for degree in range(ORDERS):
        for peer in range(peers):
            gathered[pl.ds(peer * cap, cap), :] = received[pl.ds(peer * block + degree, cap, stride=ORDERS), :]
        high, low = two_parts(gathered[...])
        out[degree] = jnp.dot(hits, high, preferred_element_type=F32) + jnp.dot(
            hits, low, preferred_element_type=F32
        )


def collect(received, rows, peers, cap):
    faces = received.shape[1]
    return pl.pallas_call(
        functools.partial(collect_body, peers, cap),
        out_shape=jax.ShapeDtypeStruct((ORDERS, rows, faces), F32),
        in_specs=[IN_VMEM],
        out_specs=IN_VMEM,
        scratch_shapes=[pltpu.VMEM((peers * cap, faces), F32)],
        compiler_params=pltpu.CompilerParams(vmem_limit_bytes=KERNEL_VMEM),
        name="collect",
    )(received)


def interface_body(before, edge, ghost, out, result, sems):
    rows = ghost.shape[1]
    tiles = sems.shape[0]
    tile = rows // tiles
    layer = jnp.where(lax.axis_index("region") == 0, out.shape[1] - 1, 0)

    def store(step):
        part = pl.ds(step * tile, tile)
        return pltpu.make_async_copy(result.at[:, part], out.at[:, layer, part], sems.at[step])

    for step in range(tiles):
        part = pl.ds(step * tile, tile)
        share = edge[ORDERS, part]
        moment = [edge[degree, part] + share * ghost[degree, part] for degree in range(ORDERS)]
        updated = sources(moment, edge[ORDERS + 1, part])
        for degree in range(ORDERS):
            result[degree, part] = updated[degree]
        store(step).start()
    for step in range(tiles):
        store(step).wait()


def interface_update(before, edge, ghost):
    rows, faces = ghost.shape[1:]
    tiles = rows // TILE
    return pl.pallas_call(
        interface_body,
        out_shape=jax.ShapeDtypeStruct(before.shape, F32),
        in_specs=[IN_HBM, IN_VMEM, IN_VMEM],
        out_specs=IN_HBM,
        scratch_shapes=[pltpu.VMEM((ORDERS, rows, faces), F32), pltpu.SemaphoreType.DMA((tiles,))],
        input_output_aliases={0: 0},
        compiler_params=pltpu.CompilerParams(vmem_limit_bytes=KERNEL_VMEM),
        name="interface_update",
    )(before, edge, ghost)


def on_device(
    moments, courant_azimuth, courant_radial, courant_axial, shear, owner, target, ami_weight
):
    moment = moments[0]
    rows, faces = moment.shape[2], moment.shape[3]
    peers = lax.axis_size("cells")
    regions = lax.axis_size("region")
    cap = max(2, 2 * rows // peers)
    payload, tail = dispatch(owner[0, :, 0], target[0], moment, ami_weight[0], peers, cap)
    received = lax.all_to_all(
        payload.reshape(peers, 1, -1), "cells", split_axis=0, concat_axis=0, tiled=True
    )
    rim = lax.ppermute(tail, "cells", [(i, (i + 1) % peers) for i in range(peers)])
    rim = rim.reshape(ORDERS, -1, rows)
    before, edge = local_update(
        moment, rim[..., None], courant_azimuth[0], courant_radial[0], courant_axial[0], shear[0]
    )
    other = collect(received.reshape(-1, faces), rows, peers, cap)
    ghost = lax.ppermute(other, "region", [(i, regions - 1 - i) for i in range(regions)])
    updated = interface_update(before, edge, ghost)
    return updated[None]


def solution(mesh):
    field = P("region", None, None, "cells")
    cells = P("region", None, None, None, "cells")
    return jax.shard_map(
        on_device,
        mesh=mesh,
        in_specs=(
            cells,
            field,
            field,
            field,
            field,
            P("region", "cells", None),
            P("region", "cells"),
            P("region", "cells", None, None),
        ),
        out_specs=cells,
        check_vma=False,
    )
```

time: 76.5 us -> 58.6 us (0.77)
  the two profiles are of different devices: /device:TPU:1 before, /device:TPU:0 now
where the time goes in v1:
time: 58.6 us; the launch traced here: 58.2 us
  blocking collectives  29.8 us (51%)
  Pallas kernels  18.3 us (31%)
  waiting for transfers between devices  6.73 us (11%)
  local copies, waits for them, and re-layouts  2.71 us (5%)
  starting transfers between devices  0.69 us (1%)
    all_to_all x1, blocking collectives, on_device(): lax.all_to_all(payload.reshape(peers, 1, -1), 'cells', split_axis=0, conc...  29.8 us
    pallas_call x1, Pallas kernels, local_update(): pl.pallas_call(local_body, out_shape=(jax.ShapeDtypeStruct(moments.shape,...  8.47 us
    pallas_call x1, Pallas kernels, dispatch(): pl.pallas_call(functools.partial(dispatch_body, cap), out_shape=(jax.Shap...  7.9 us
    ppermute x1, waiting for transfers between devices, on_device(): lax.ppermute(tail, 'cells', [(i, (i + 1) % peers) for i in range(peers)])  6.73 us
    another operation x1, local copies, waits for them, and re-layouts, on_device(): rim[..., None]  1.67 us
    pallas_call x1, Pallas kernels, interface_update(): pl.pallas_call(interface_body, out_shape=jax.ShapeDtypeStruct(before.shap...  1.56 us
  transfers between devices with their start and end apart: 2, of which 1 were waited for; matrix products, arithmetic and copies ran while one was open for 3% of the time, Pallas kernels for 15%

profile of v1, /device:TPU:0, one launch (start us, length us, event | category | flops | bytes accessed | tf_op | source)
XLA Modules:
  0.0 58.2 jit_solution(10272791754377569835)
XLA Ops:
  0.0 7.9 %dispatch.1 = (f32[1552,128]{1,0:T(8,128)}, f32[24,128]{1,0:T(8,128)}) custom-call(s32[128]{0:T(128)} %bitcast.22, s32[128]{0:T(128)} %bitcast.23, f32[6,4,128,128]{3,2,1,0:T(8,128)} %bitcast.14, f32[128,128,128]{2,1,0:T(8,128)} %bitcast.13), custom_call_target="tpu_custom_call" | custom-call | tf_op jit(solution)/shard_map/dispatch/pallas_call | solution.py:230
  7.9 0.0 copy-start.1
  7.9 29.8 %all_to_all.5 = f32[16,1,12416]{2,1,0:T(1,128)S(1)} all-to-all(f32[16,1,12416]{2,1,0:T(1,128)} %bitcast.16), channel_id=1, replica_groups=mesh['region'=2,'cells'=16] {'cells'}, dimensions={0} | all-to-all | bytes 1589248 | tf_op jit(solution)/shard_map/all_to_all | solution.py:432
  37.7 0.4 collect.1
  38.1 0.1 collective-permute-start.1
  38.1 0.0 copy-done.1
  38.1 0.6 %collective-permute-start = (f32[24,128]{1,0:T(8,128)S(1)}, f32[24,128]{1,0:T(8,128)S(1)}, u32[]{:S(2)}, u32[]{:S(2)}) collective-permute-start(f32[24,128]{1,0:T(8,128)S(1)} %copy-done.1), channel_id=1, source_target_pairs={{0,1},{1,2},{2,3},{3,4},{4,5},{5,6},{6,7},{7,8},{8,9},{9,10},{10,1... | collective-permute-start | bytes 36872 | tf_op jit(solution)/shard_map/ppermute | solution.py:435
  38.8 6.7 %collective-permute-done = f32[24,128]{1,0:T(8,128)S(1)} collective-permute-done((f32[24,128]{1,0:T(8,128)S(1)}, f32[24,128]{1,0:T(8,128)S(1)}, u32[]{:S(2)}, u32[]{:S(2)}) %collective-permute-start) | collective-permute-done | bytes 12320 | tf_op jit(solution)/shard_map/ppermute | solution.py:435
  45.5 1.7 %copy.11.rim = f32[6,4,128,1]{3,2,1,0:T(8,128)} copy(f32[6,4,128,1]{2,1,0,3:T(4,128)S(1)} %bitcast.21) | data formatting | bytes 24576 | tf_op jit(solution)/shard_map/broadcast_in_dim;reshape | solution.py:438
  47.2 8.5 %local_update.1 = (f32[6,4,128,128]{3,2,1,0:T(8,128)}, f32[8,128,128]{2,1,0:T(8,128)}) custom-call(f32[6,4,128,128]{3,2,1,0:T(8,128)} %bitcast.15, f32[6,4,128,1]{3,2,1,0:T(8,128)} %copy.11.rim, f32[4,128,128]{2,1,0:T(8,128)} %bitcast.17, f32[4,128,128]{2,1,0:T(8,128)} %bitcast.18, f32[4,128,128]{2,1,0:T(8,128)} %bitcast.19, f32[4,128,128]{2,1,0:T(8,128)} %bitcast.20), custom_call_target="tpu_custom_call" | custom-call | tf_op jit(solution)/shard_map/local_update/pallas_call | solution.py:331
  55.6 0.0 collective-permute-done.1.ghost
  55.6 0.0 copy-start
  55.7 1.0 %copy-done = f32[8,128,128]{2,1,0:T(8,128)S(1)} copy-done((f32[8,128,128]{2,1,0:T(8,128)S(1)}, f32[8,128,128]{2,1,0:T(8,128)}, u32[]{:S(2)}) %copy-start) | copy-done | bytes 524312
  56.7 1.6 %interface_update.1 = f32[6,4,128,128]{3,2,1,0:T(8,128)} custom-call(f32[6,4,128,128]{3,2,1,0:T(8,128)} %get-tuple-element.10.before, f32[8,128,128]{2,1,0:T(8,128)S(1)} %copy-done, f32[6,128,128]{2,1,0:T(8,128)S(1)} %collective-permute-done.1.ghost), custom_call_target="tpu_custom_call", output_to_operand_aliasing={{}: (0, {})} | custom-call | tf_op jit(solution)/shard_map/interface_update/pallas_call | solution.py:411
Async XLA Ops:
  7.9 30.2 %copy-start.1 = (f32[24,128]{1,0:T(8,128)S(1)}, f32[24,128]{1,0:T(8,128)}, u32[]{:S(2)}) copy-start(f32[24,128]{1,0:T(8,128)} %get-tuple-element.9) | copy-start | bytes 36868
  38.1 17.6 %collective-permute-start.1 = (f32[6,128,128]{2,1,0:T(8,128)S(1)}, f32[6,128,128]{2,1,0:T(8,128)S(1)}, u32[]{:S(2)}, u32[]{:S(2)}) collective-permute-start(f32[6,128,128]{2,1,0:T(8,128)S(1)} %collect.1), channel_id=1, source_target_pairs={{0,16},{16,0},{1,17},{17,1},{2,18},{18,2},{3,19},{19,3},{4,20},{20... | collective-permute-start | bytes 1179656 | tf_op jit(solution)/shard_map/ppermute | solution.py:441
  38.1 7.3 %collective-permute-start = (f32[24,128]{1,0:T(8,128)S(1)}, f32[24,128]{1,0:T(8,128)S(1)}, u32[]{:S(2)}, u32[]{:S(2)}) collective-permute-start(f32[24,128]{1,0:T(8,128)S(1)} %copy-done.1), channel_id=1, source_target_pairs={{0,1},{1,2},{2,3},{3,4},{4,5},{5,6},{6,7},{7,8},{8,9},{9,10},{10,1... | collective-permute-start | bytes 36872 | tf_op jit(solution)/shard_map/ppermute | solution.py:435
  55.6 1.0 %copy-start = (f32[8,128,128]{2,1,0:T(8,128)S(1)}, f32[8,128,128]{2,1,0:T(8,128)}, u32[]{:S(2)}) copy-start(f32[8,128,128]{2,1,0:T(8,128)} %get-tuple-element.11.edge) | copy-start | bytes 1572868

commit v2 on v1

--- a/solution.py
+++ b/solution.py
@@ -19,7 +19,9 @@
 GROUP = 8
 TILE = 32
 FULL_VMEM = 58 * 1024 * 1024
-BOUNDS = (0, 4, 8, 12, 14, 16)
+BOUNDS = (0, 2, 5, 8, 11, 14, 16)
+AHEAD = 3
+RIM_STEP = 3
 IN_VMEM = pl.BlockSpec(memory_space=pltpu.VMEM)
 IN_HBM = pl.BlockSpec(memory_space=pltpu.HBM)
 
@@ -148,11 +150,6 @@
     layer_copy(0).start()
     for copy in index_copies:
         copy.start()
-    for step in range(len(BOUNDS) - 1):
-        weight_copy(step).start()
-        if step == 0:
-            for index in range(1, layers):
-                layer_copy(index).start()
 
     out[...] = jnp.zeros_like(out)
     lane = lax.broadcasted_iota(jnp.int32, (1, faces), 1)
@@ -166,6 +163,8 @@
 
     source[pl.ds(ORDERS * rows, (PAD - ORDERS) * rows)] = jnp.zeros(((PAD - ORDERS) * rows, faces), F32)
     layer_copy(0).wait()
+    for step in range(AHEAD):
+        weight_copy(step).start()
     for degree in range(ORDERS):
         source[pl.ds(degree * rows, rows)] = moments[degree, layer]
     for copy in index_copies:
@@ -193,6 +192,11 @@
     pending = []
     for step in range(len(BOUNDS) - 1):
         weight_copy(step).wait()
+        if step + AHEAD < len(BOUNDS) - 1:
+            weight_copy(step + AHEAD).start()
+        if step == 0:
+            for index in range(1, layers):
+                layer_copy(index).start()
         products = []
         for group in range(BOUNDS[step], BOUNDS[step + 1]):
             first = group * GROUP
@@ -205,7 +209,7 @@
             products.append((first, product))
             if pending:
                 place(*pending.pop(0))
-        if step == 0:
+        if step == RIM_STEP:
             for index in range(1, layers):
                 layer_copy(index).wait()
             tail = jnp.zeros((rows, faces), F32)
@@ -383,6 +387,24 @@
     )(received)
 
 
+def fetch_body(source, out, sem):
+    copy = pltpu.make_async_copy(source, out, sem)
+    copy.start()
+    copy.wait()
+
+
+def fetch(edge):
+    return pl.pallas_call(
+        fetch_body,
+        out_shape=jax.ShapeDtypeStruct(edge.shape, F32),
+        in_specs=[IN_HBM],
+        out_specs=IN_VMEM,
+        scratch_shapes=[pltpu.SemaphoreType.DMA],
+        compiler_params=pltpu.CompilerParams(vmem_limit_bytes=KERNEL_VMEM),
+        name="fetch",
+    )(edge)
+
+
 def interface_body(before, edge, ghost, out, result, sems):
     rows = ghost.shape[1]
     tiles = sems.shape[0]
@@ -439,6 +461,7 @@
     )
     other = collect(received.reshape(-1, faces), rows, peers, cap)
     ghost = lax.ppermute(other, "region", [(i, regions - 1 - i) for i in range(regions)])
+    edge = fetch(edge)
     updated = interface_update(before, edge, ghost)
     return updated[None]
 

time: 58.6 us -> 57.9 us (0.988)
  Pallas kernels: 18.3 us -> 17.5 us
    pallas_call x1, Pallas kernels: 7.9 us -> 7.09 us  [dispatch(): pl.pallas_call(functools.partial(dispatch_body, cap), out_shape=(jax.Shap...]
where the time goes in v2:
time: 57.9 us; the launch traced here: 57.5 us
  blocking collectives  29.8 us (51%)
  Pallas kernels  17.5 us (30%)
  waiting for transfers between devices  6.73 us (12%)
  local copies, waits for them, and re-layouts  2.71 us (5%)
  starting transfers between devices  0.69 us (1%)
    all_to_all x1, blocking collectives, on_device(): lax.all_to_all(payload.reshape(peers, 1, -1), 'cells', split_axis=0, conc...  29.8 us
    pallas_call x1, Pallas kernels, local_update(): pl.pallas_call(local_body, out_shape=(jax.ShapeDtypeStruct(moments.shape,...  8.47 us
    pallas_call x1, Pallas kernels, dispatch(): pl.pallas_call(functools.partial(dispatch_body, cap), out_shape=(jax.Shap...  7.09 us
    ppermute x1, waiting for transfers between devices, on_device(): lax.ppermute(tail, 'cells', [(i, (i + 1) % peers) for i in range(peers)])  6.73 us
    another operation x1, local copies, waits for them, and re-layouts, on_device(): rim[..., None]  1.67 us
    pallas_call x1, Pallas kernels, interface_update(): pl.pallas_call(interface_body, out_shape=jax.ShapeDtypeStruct(before.shap...  1.56 us
  transfers between devices with their start and end apart: 2, of which 1 were waited for; matrix products, arithmetic and copies ran while one was open for 3% of the time, Pallas kernels for 15%

profile of v2, /device:TPU:0, one launch (start us, length us, event | category | flops | bytes accessed | tf_op | source)
XLA Modules:
  0.0 57.5 jit_solution(2110929403926170339)
XLA Ops:
  0.0 7.1 %dispatch.1 = (f32[1552,128]{1,0:T(8,128)}, f32[24,128]{1,0:T(8,128)}) custom-call(s32[128]{0:T(128)} %bitcast.22, s32[128]{0:T(128)} %bitcast.23, f32[6,4,128,128]{3,2,1,0:T(8,128)} %bitcast.14, f32[128,128,128]{2,1,0:T(8,128)} %bitcast.13), custom_call_target="tpu_custom_call" | custom-call | tf_op jit(solution)/shard_map/dispatch/pallas_call | solution.py:234
  7.1 0.0 copy-start.1
  7.1 29.8 %all_to_all.5 = f32[16,1,12416]{2,1,0:T(1,128)S(1)} all-to-all(f32[16,1,12416]{2,1,0:T(1,128)} %bitcast.16), channel_id=1, replica_groups=mesh['region'=2,'cells'=16] {'cells'}, dimensions={0} | all-to-all | bytes 1589248 | tf_op jit(solution)/shard_map/all_to_all | solution.py:454
  36.9 0.4 collect.1
  37.3 0.1 collective-permute-start.1
  37.3 0.0 copy-done.1
  37.3 0.6 %collective-permute-start = (f32[24,128]{1,0:T(8,128)S(1)}, f32[24,128]{1,0:T(8,128)S(1)}, u32[]{:S(2)}, u32[]{:S(2)}) collective-permute-start(f32[24,128]{1,0:T(8,128)S(1)} %copy-done.1), channel_id=1, source_target_pairs={{0,1},{1,2},{2,3},{3,4},{4,5},{5,6},{6,7},{7,8},{8,9},{9,10},{10,1... | collective-permute-start | bytes 36872 | tf_op jit(solution)/shard_map/ppermute | solution.py:457
  38.0 6.7 %collective-permute-done = f32[24,128]{1,0:T(8,128)S(1)} collective-permute-done((f32[24,128]{1,0:T(8,128)S(1)}, f32[24,128]{1,0:T(8,128)S(1)}, u32[]{:S(2)}, u32[]{:S(2)}) %collective-permute-start) | collective-permute-done | bytes 12320 | tf_op jit(solution)/shard_map/ppermute | solution.py:457
  44.7 1.7 %copy.11.rim = f32[6,4,128,1]{3,2,1,0:T(8,128)} copy(f32[6,4,128,1]{2,1,0,3:T(4,128)S(1)} %bitcast.21) | data formatting | bytes 24576 | tf_op jit(solution)/shard_map/broadcast_in_dim;reshape | solution.py:460
  46.4 8.5 %local_update.1 = (f32[6,4,128,128]{3,2,1,0:T(8,128)}, f32[8,128,128]{2,1,0:T(8,128)}) custom-call(f32[6,4,128,128]{3,2,1,0:T(8,128)} %bitcast.15, f32[6,4,128,1]{3,2,1,0:T(8,128)} %copy.11.rim, f32[4,128,128]{2,1,0:T(8,128)} %bitcast.17, f32[4,128,128]{2,1,0:T(8,128)} %bitcast.18, f32[4,128,128]{2,1,0:T(8,128)} %bitcast.19, f32[4,128,128]{2,1,0:T(8,128)} %bitcast.20), custom_call_target="tpu_custom_call" | custom-call | tf_op jit(solution)/shard_map/local_update/pallas_call | solution.py:335
  54.8 0.0 copy-start
  54.9 1.0 %copy-done = f32[8,128,128]{2,1,0:T(8,128)S(1)} copy-done((f32[8,128,128]{2,1,0:T(8,128)S(1)}, f32[8,128,128]{2,1,0:T(8,128)}, u32[]{:S(2)}) %copy-start) | copy-done | bytes 524312
  55.9 0.0 collective-permute-done.1.ghost
  56.0 1.6 %interface_update.1 = f32[6,4,128,128]{3,2,1,0:T(8,128)} custom-call(f32[6,4,128,128]{3,2,1,0:T(8,128)} %get-tuple-element.10.before, f32[8,128,128]{2,1,0:T(8,128)S(1)} %fetch.1.edge, f32[6,128,128]{2,1,0:T(8,128)S(1)} %collective-permute-done.1.ghost), custom_call_target="tpu_custom_call", output_to_operand_aliasing={{}: (0, {})} | custom-call | tf_op jit(solution)/shard_map/interface_update/pallas_call | solution.py:433
  (1 shorter events, 0.0 us)
Async XLA Ops:
  7.1 30.2 %copy-start.1 = (f32[24,128]{1,0:T(8,128)S(1)}, f32[24,128]{1,0:T(8,128)}, u32[]{:S(2)}) copy-start(f32[24,128]{1,0:T(8,128)} %get-tuple-element.9) | copy-start | bytes 36868
  37.3 18.7 %collective-permute-start.1 = (f32[6,128,128]{2,1,0:T(8,128)S(1)}, f32[6,128,128]{2,1,0:T(8,128)S(1)}, u32[]{:S(2)}, u32[]{:S(2)}) collective-permute-start(f32[6,128,128]{2,1,0:T(8,128)S(1)} %collect.1), channel_id=1, source_target_pairs={{0,16},{16,0},{1,17},{17,1},{2,18},{18,2},{3,19},{19,3},{4,20},{20... | collective-permute-start | bytes 1179656 | tf_op jit(solution)/shard_map/ppermute | solution.py:463
  37.3 7.3 %collective-permute-start = (f32[24,128]{1,0:T(8,128)S(1)}, f32[24,128]{1,0:T(8,128)S(1)}, u32[]{:S(2)}, u32[]{:S(2)}) collective-permute-start(f32[24,128]{1,0:T(8,128)S(1)} %copy-done.1), channel_id=1, source_target_pairs={{0,1},{1,2},{2,3},{3,4},{4,5},{5,6},{6,7},{7,8},{8,9},{9,10},{10,1... | collective-permute-start | bytes 36872 | tf_op jit(solution)/shard_map/ppermute | solution.py:457
  54.8 1.0 %copy-start = (f32[8,128,128]{2,1,0:T(8,128)S(1)}, f32[8,128,128]{2,1,0:T(8,128)}, u32[]{:S(2)}) copy-start(f32[8,128,128]{2,1,0:T(8,128)} %get-tuple-element.11.source) | copy-start | bytes 1572868

commit v3 on v2

--- a/solution.py
+++ b/solution.py
@@ -18,6 +18,7 @@
 PAD = 8
 GROUP = 8
 TILE = 32
+EDGE_TILE = 32
 FULL_VMEM = 58 * 1024 * 1024
 BOUNDS = (0, 2, 5, 8, 11, 14, 16)
 AHEAD = 3
@@ -148,6 +149,8 @@
         pltpu.make_async_copy(target_hbm, target, index_sem.at[1]),
     )
     layer_copy(0).start()
+    for step in range(AHEAD):
+        weight_copy(step).start(priority=1)
     for copy in index_copies:
         copy.start()
 
@@ -163,8 +166,6 @@
 
     source[pl.ds(ORDERS * rows, (PAD - ORDERS) * rows)] = jnp.zeros(((PAD - ORDERS) * rows, faces), F32)
     layer_copy(0).wait()
-    for step in range(AHEAD):
-        weight_copy(step).start()
     for degree in range(ORDERS):
         source[pl.ds(degree * rows, rows)] = moments[degree, layer]
     for copy in index_copies:
@@ -429,7 +430,7 @@
 
 def interface_update(before, edge, ghost):
     rows, faces = ghost.shape[1:]
-    tiles = rows // TILE
+    tiles = rows // EDGE_TILE
     return pl.pallas_call(
         interface_body,
         out_shape=jax.ShapeDtypeStruct(before.shape, F32),

time: 57.9 us -> 57.1 us (0.986)
  Pallas kernels: 17.5 us -> 16.8 us
    pallas_call x1, Pallas kernels: 7.09 us -> 6.34 us  [dispatch(): pl.pallas_call(functools.partial(dispatch_body, cap), out_shape=(jax.Shap...]
where the time goes in v3:
time: 57.1 us; the launch traced here: 56.8 us
  blocking collectives  29.8 us (52%)
  Pallas kernels  16.8 us (29%)
  waiting for transfers between devices  6.73 us (12%)
  local copies, waits for them, and re-layouts  2.71 us (5%)
  starting transfers between devices  0.69 us (1%)
    all_to_all x1, blocking collectives, on_device(): lax.all_to_all(payload.reshape(peers, 1, -1), 'cells', split_axis=0, conc...  29.8 us
    pallas_call x1, Pallas kernels, local_update(): pl.pallas_call(local_body, out_shape=(jax.ShapeDtypeStruct(moments.shape,...  8.47 us
    ppermute x1, waiting for transfers between devices, on_device(): lax.ppermute(tail, 'cells', [(i, (i + 1) % peers) for i in range(peers)])  6.73 us
    pallas_call x1, Pallas kernels, dispatch(): pl.pallas_call(functools.partial(dispatch_body, cap), out_shape=(jax.Shap...  6.34 us
    another operation x1, local copies, waits for them, and re-layouts, on_device(): rim[..., None]  1.67 us
    pallas_call x1, Pallas kernels, interface_update(): pl.pallas_call(interface_body, out_shape=jax.ShapeDtypeStruct(before.shap...  1.56 us
  transfers between devices with their start and end apart: 2, of which 1 were waited for; matrix products, arithmetic and copies ran while one was open for 3% of the time, Pallas kernels for 15%

profile of v3, /device:TPU:0, one launch (start us, length us, event | category | flops | bytes accessed | tf_op | source)
XLA Modules:
  0.0 56.8 jit_solution(16695688963901354627)
XLA Ops:
  0.0 6.3 %dispatch.1 = (f32[1552,128]{1,0:T(8,128)}, f32[24,128]{1,0:T(8,128)}) custom-call(s32[128]{0:T(128)} %bitcast.22, s32[128]{0:T(128)} %bitcast.23, f32[6,4,128,128]{3,2,1,0:T(8,128)} %bitcast.14, f32[128,128,128]{2,1,0:T(8,128)} %bitcast.13), custom_call_target="tpu_custom_call" | custom-call | tf_op jit(solution)/shard_map/dispatch/pallas_call | solution.py:235
  6.4 0.0 copy-start.1
  6.4 29.8 %all_to_all.5 = f32[16,1,12416]{2,1,0:T(1,128)S(1)} all-to-all(f32[16,1,12416]{2,1,0:T(1,128)} %bitcast.16), channel_id=1, replica_groups=mesh['region'=2,'cells'=16] {'cells'}, dimensions={0} | all-to-all | bytes 1589248 | tf_op jit(solution)/shard_map/all_to_all | solution.py:455
  36.2 0.4 collect.1
  36.5 0.1 collective-permute-start.1
  36.6 0.0 copy-done.1
  36.6 0.6 %collective-permute-start = (f32[24,128]{1,0:T(8,128)S(1)}, f32[24,128]{1,0:T(8,128)S(1)}, u32[]{:S(2)}, u32[]{:S(2)}) collective-permute-start(f32[24,128]{1,0:T(8,128)S(1)} %copy-done.1), channel_id=1, source_target_pairs={{0,1},{1,2},{2,3},{3,4},{4,5},{5,6},{6,7},{7,8},{8,9},{9,10},{10,1... | collective-permute-start | bytes 36872 | tf_op jit(solution)/shard_map/ppermute | solution.py:458
  37.2 6.7 %collective-permute-done = f32[24,128]{1,0:T(8,128)S(1)} collective-permute-done((f32[24,128]{1,0:T(8,128)S(1)}, f32[24,128]{1,0:T(8,128)S(1)}, u32[]{:S(2)}, u32[]{:S(2)}) %collective-permute-start) | collective-permute-done | bytes 12320 | tf_op jit(solution)/shard_map/ppermute | solution.py:458
  44.0 1.7 %copy.11.rim = f32[6,4,128,1]{3,2,1,0:T(8,128)} copy(f32[6,4,128,1]{2,1,0,3:T(4,128)S(1)} %bitcast.21) | data formatting | bytes 24576 | tf_op jit(solution)/shard_map/broadcast_in_dim;reshape | solution.py:461
  45.6 8.5 %local_update.1 = (f32[6,4,128,128]{3,2,1,0:T(8,128)}, f32[8,128,128]{2,1,0:T(8,128)}) custom-call(f32[6,4,128,128]{3,2,1,0:T(8,128)} %bitcast.15, f32[6,4,128,1]{3,2,1,0:T(8,128)} %copy.11.rim, f32[4,128,128]{2,1,0:T(8,128)} %bitcast.17, f32[4,128,128]{2,1,0:T(8,128)} %bitcast.18, f32[4,128,128]{2,1,0:T(8,128)} %bitcast.19, f32[4,128,128]{2,1,0:T(8,128)} %bitcast.20), custom_call_target="tpu_custom_call" | custom-call | tf_op jit(solution)/shard_map/local_update/pallas_call | solution.py:336
  54.1 0.0 copy-start
  54.1 1.0 %copy-done = f32[8,128,128]{2,1,0:T(8,128)S(1)} copy-done((f32[8,128,128]{2,1,0:T(8,128)S(1)}, f32[8,128,128]{2,1,0:T(8,128)}, u32[]{:S(2)}) %copy-start) | copy-done | bytes 524312
  55.2 0.0 collective-permute-done.1.ghost
  55.2 1.6 %interface_update.1 = f32[6,4,128,128]{3,2,1,0:T(8,128)} custom-call(f32[6,4,128,128]{3,2,1,0:T(8,128)} %get-tuple-element.10.before, f32[8,128,128]{2,1,0:T(8,128)S(1)} %fetch.1.edge, f32[6,128,128]{2,1,0:T(8,128)S(1)} %collective-permute-done.1.ghost), custom_call_target="tpu_custom_call", output_to_operand_aliasing={{}: (0, {})} | custom-call | tf_op jit(solution)/shard_map/interface_update/pallas_call | solution.py:434
  (1 shorter events, 0.0 us)
Async XLA Ops:
  6.4 30.2 %copy-start.1 = (f32[24,128]{1,0:T(8,128)S(1)}, f32[24,128]{1,0:T(8,128)}, u32[]{:S(2)}) copy-start(f32[24,128]{1,0:T(8,128)} %get-tuple-element.9) | copy-start | bytes 36868
  36.5 18.7 %collective-permute-start.1 = (f32[6,128,128]{2,1,0:T(8,128)S(1)}, f32[6,128,128]{2,1,0:T(8,128)S(1)}, u32[]{:S(2)}, u32[]{:S(2)}) collective-permute-start(f32[6,128,128]{2,1,0:T(8,128)S(1)} %collect.1), channel_id=1, source_target_pairs={{0,16},{16,0},{1,17},{17,1},{2,18},{18,2},{3,19},{19,3},{4,20},{20... | collective-permute-start | bytes 1179656 | tf_op jit(solution)/shard_map/ppermute | solution.py:464
  36.6 7.3 %collective-permute-start = (f32[24,128]{1,0:T(8,128)S(1)}, f32[24,128]{1,0:T(8,128)S(1)}, u32[]{:S(2)}, u32[]{:S(2)}) collective-permute-start(f32[24,128]{1,0:T(8,128)S(1)} %copy-done.1), channel_id=1, source_target_pairs={{0,1},{1,2},{2,3},{3,4},{4,5},{5,6},{6,7},{7,8},{8,9},{9,10},{10,1... | collective-permute-start | bytes 36872 | tf_op jit(solution)/shard_map/ppermute | solution.py:458
  54.1 1.0 %copy-start = (f32[8,128,128]{2,1,0:T(8,128)S(1)}, f32[8,128,128]{2,1,0:T(8,128)}, u32[]{:S(2)}) copy-start(f32[8,128,128]{2,1,0:T(8,128)} %get-tuple-element.11.source) | copy-start | bytes 1572868

commit v4 on v3

--- a/solution.py
+++ b/solution.py
@@ -172,11 +172,16 @@
         copy.wait()
     width = PAD * GROUP
     column = (lax.broadcasted_iota(jnp.int32, (faces, 2 * width), 1) % width) // PAD
-    turned = []
-    for first in range(0, rows, GROUP):
-        value = jnp.concatenate([source[pl.ds(first + i, PAD, stride=rows)] for i in range(GROUP)], axis=0)
-        high = value.astype(BF16).astype(F32)
-        turned.append(jnp.concatenate([high, value - high], axis=0).T)
+    turned = {}
+
+    def turn(step):
+        for group in range(BOUNDS[step], BOUNDS[step + 1]):
+            first = group * GROUP
+            value = jnp.concatenate([source[pl.ds(first + i, PAD, stride=rows)] for i in range(GROUP)], axis=0)
+            high = value.astype(BF16).astype(F32)
+            turned[group] = jnp.concatenate([high, value - high], axis=0).T
+
+    turn(0)
 
     def place(first, product):
         product = product.T
@@ -198,6 +203,8 @@
         if step == 0:
             for index in range(1, layers):
                 layer_copy(index).start()
+        if step + 1 < len(BOUNDS) - 1:
+            turn(step + 1)
         products = []
         for group in range(BOUNDS[step], BOUNDS[step + 1]):
             first = group * GROUP

time: 57.1 us -> 57 us (level)
  no operation moved by 1% of the time
where the time goes in v4:
time: 57 us; the launch traced here: 56.7 us
  blocking collectives  29.8 us (52%)
  Pallas kernels  16.7 us (29%)
  waiting for transfers between devices  6.73 us (12%)
  local copies, waits for them, and re-layouts  2.71 us (5%)
  starting transfers between devices  0.69 us (1%)
    all_to_all x1, blocking collectives, on_device(): lax.all_to_all(payload.reshape(peers, 1, -1), 'cells', split_axis=0, conc...  29.8 us
    pallas_call x1, Pallas kernels, local_update(): pl.pallas_call(local_body, out_shape=(jax.ShapeDtypeStruct(moments.shape,...  8.47 us
    ppermute x1, waiting for transfers between devices, on_device(): lax.ppermute(tail, 'cells', [(i, (i + 1) % peers) for i in range(peers)])  6.73 us
    pallas_call x1, Pallas kernels, dispatch(): pl.pallas_call(functools.partial(dispatch_body, cap), out_shape=(jax.Shap...  6.26 us
    another operation x1, local copies, waits for them, and re-layouts, on_device(): rim[..., None]  1.67 us
    pallas_call x1, Pallas kernels, interface_update(): pl.pallas_call(interface_body, out_shape=jax.ShapeDtypeStruct(before.shap...  1.56 us
  transfers between devices with their start and end apart: 2, of which 1 were waited for; matrix products, arithmetic and copies ran while one was open for 3% of the time, Pallas kernels for 15%

profile of v4, /device:TPU:0, one launch (start us, length us, event | category | flops | bytes accessed | tf_op | source)
XLA Modules:
  0.0 56.7 jit_solution(18111627500430467959)
XLA Ops:
  0.0 6.3 %dispatch.1 = (f32[1552,128]{1,0:T(8,128)}, f32[24,128]{1,0:T(8,128)}) custom-call(s32[128]{0:T(128)} %bitcast.22, s32[128]{0:T(128)} %bitcast.23, f32[6,4,128,128]{3,2,1,0:T(8,128)} %bitcast.14, f32[128,128,128]{2,1,0:T(8,128)} %bitcast.13), custom_call_target="tpu_custom_call" | custom-call | tf_op jit(solution)/shard_map/dispatch/pallas_call | solution.py:242
  6.3 0.0 copy-start.1
  6.3 29.8 %all_to_all.5 = f32[16,1,12416]{2,1,0:T(1,128)S(1)} all-to-all(f32[16,1,12416]{2,1,0:T(1,128)} %bitcast.16), channel_id=1, replica_groups=mesh['region'=2,'cells'=16] {'cells'}, dimensions={0} | all-to-all | bytes 1589248 | tf_op jit(solution)/shard_map/all_to_all | solution.py:462
  36.1 0.4 collect.1
  36.4 0.1 collective-permute-start.1
  36.5 0.0 copy-done.1
  36.5 0.6 %collective-permute-start = (f32[24,128]{1,0:T(8,128)S(1)}, f32[24,128]{1,0:T(8,128)S(1)}, u32[]{:S(2)}, u32[]{:S(2)}) collective-permute-start(f32[24,128]{1,0:T(8,128)S(1)} %copy-done.1), channel_id=1, source_target_pairs={{0,1},{1,2},{2,3},{3,4},{4,5},{5,6},{6,7},{7,8},{8,9},{9,10},{10,1... | collective-permute-start | bytes 36872 | tf_op jit(solution)/shard_map/ppermute | solution.py:465
  37.1 6.7 %collective-permute-done = f32[24,128]{1,0:T(8,128)S(1)} collective-permute-done((f32[24,128]{1,0:T(8,128)S(1)}, f32[24,128]{1,0:T(8,128)S(1)}, u32[]{:S(2)}, u32[]{:S(2)}) %collective-permute-start) | collective-permute-done | bytes 12320 | tf_op jit(solution)/shard_map/ppermute | solution.py:465
  43.9 1.7 %copy.11.rim = f32[6,4,128,1]{3,2,1,0:T(8,128)} copy(f32[6,4,128,1]{2,1,0,3:T(4,128)S(1)} %bitcast.21) | data formatting | bytes 24576 | tf_op jit(solution)/shard_map/broadcast_in_dim;reshape | solution.py:468
  45.5 8.5 %local_update.1 = (f32[6,4,128,128]{3,2,1,0:T(8,128)}, f32[8,128,128]{2,1,0:T(8,128)}) custom-call(f32[6,4,128,128]{3,2,1,0:T(8,128)} %bitcast.15, f32[6,4,128,1]{3,2,1,0:T(8,128)} %copy.11.rim, f32[4,128,128]{2,1,0:T(8,128)} %bitcast.17, f32[4,128,128]{2,1,0:T(8,128)} %bitcast.18, f32[4,128,128]{2,1,0:T(8,128)} %bitcast.19, f32[4,128,128]{2,1,0:T(8,128)} %bitcast.20), custom_call_target="tpu_custom_call" | custom-call | tf_op jit(solution)/shard_map/local_update/pallas_call | solution.py:343
  54.0 0.0 copy-start
  54.0 1.0 %copy-done = f32[8,128,128]{2,1,0:T(8,128)S(1)} copy-done((f32[8,128,128]{2,1,0:T(8,128)S(1)}, f32[8,128,128]{2,1,0:T(8,128)}, u32[]{:S(2)}) %copy-start) | copy-done | bytes 524312
  55.1 0.0 collective-permute-done.1.ghost
  55.1 1.6 %interface_update.1 = f32[6,4,128,128]{3,2,1,0:T(8,128)} custom-call(f32[6,4,128,128]{3,2,1,0:T(8,128)} %get-tuple-element.10.before, f32[8,128,128]{2,1,0:T(8,128)S(1)} %fetch.1.edge, f32[6,128,128]{2,1,0:T(8,128)S(1)} %collective-permute-done.1.ghost), custom_call_target="tpu_custom_call", output_to_operand_aliasing={{}: (0, {})} | custom-call | tf_op jit(solution)/shard_map/interface_update/pallas_call | solution.py:441
  (1 shorter events, 0.0 us)
Async XLA Ops:
  6.3 30.3 %copy-start.1 = (f32[24,128]{1,0:T(8,128)S(1)}, f32[24,128]{1,0:T(8,128)}, u32[]{:S(2)}) copy-start(f32[24,128]{1,0:T(8,128)} %get-tuple-element.9) | copy-start | bytes 36868
  36.4 18.7 %collective-permute-start.1 = (f32[6,128,128]{2,1,0:T(8,128)S(1)}, f32[6,128,128]{2,1,0:T(8,128)S(1)}, u32[]{:S(2)}, u32[]{:S(2)}) collective-permute-start(f32[6,128,128]{2,1,0:T(8,128)S(1)} %collect.1), channel_id=1, source_target_pairs={{0,16},{16,0},{1,17},{17,1},{2,18},{18,2},{3,19},{19,3},{4,20},{20... | collective-permute-start | bytes 1179656 | tf_op jit(solution)/shard_map/ppermute | solution.py:471
  36.5 7.3 %collective-permute-start = (f32[24,128]{1,0:T(8,128)S(1)}, f32[24,128]{1,0:T(8,128)S(1)}, u32[]{:S(2)}, u32[]{:S(2)}) collective-permute-start(f32[24,128]{1,0:T(8,128)S(1)} %copy-done.1), channel_id=1, source_target_pairs={{0,1},{1,2},{2,3},{3,4},{4,5},{5,6},{6,7},{7,8},{8,9},{9,10},{10,1... | collective-permute-start | bytes 36872 | tf_op jit(solution)/shard_map/ppermute | solution.py:465
  54.0 1.0 %copy-start = (f32[8,128,128]{2,1,0:T(8,128)S(1)}, f32[8,128,128]{2,1,0:T(8,128)}, u32[]{:S(2)}) copy-start(f32[8,128,128]{2,1,0:T(8,128)} %get-tuple-element.11.source) | copy-start | bytes 1572868
